TPU v7x, 256 devices: a whole 4x4x8 slice. The times are simulated.
256 devices in a mesh: gx: 8 (over y, core), gy: 32 (over z, x).
Axes of the slice: x: 4, y: 4, z: 8, core: 2. Of those that a mesh axis runs over, the one named last changes fastest.
Arguments:
- pressure: float32 [512, 512, 512], P('gx', 'gy'), may hold values from -6 to 6
- divergence: float32 [512, 512, 512], P('gx', 'gy'), may hold values from -6 to 6
- diagonal: float32 [512, 512, 512], P('gx', 'gy'), may hold values from 0.05 to 0.5
- normals: float32 [3, 262144], P(None, ('gx', 'gy')), may hold values from -6 to 6
- traction: float32 [3, 262144], P(None, ('gx', 'gy')), may hold values from -3 to 3
- slot_of: int32 [8, 32768], P('gx'), may hold values from 0 to 98303, as said below
- counts: int32 [256], P(('gx', 'gy')), may hold values from 0 to 3072, as said below
- previous: float32 [3, 786432], P(None, ('gx', 'gy')), may hold values from -6 to 6
- secant_v: float32 [32, 3, 786432], P(None, None, ('gx', 'gy')), may hold values from -6 to 6
- secant_w: float32 [32, 3, 786432], P(None, None, ('gx', 'gy')), may hold values from -940.60406 to 940.60406
Outputs:
- pressure_new: float32 [512, 512, 512], P('gx', 'gy')
- coupled: float32 [3, 786432], P(None, ('gx', 'gy'))
Inputs may be any that keep to these rules, and one draw needn't show every extreme that they name: Within each group (row of slot_of) the places are distinct; place o * 3072 + s has s < counts[a * 32 + o]; every such place is used; the rows of one device (aligned blocks of 1024 entries) send at most 96 rows to one owner, and exactly 96 to some owner. The counts of one group sum to 32768; some owner of every group holds exactly 3072.
All inputs are finite; a program needn't handle non-finite values.
Results may differ from a plain program's by a relative error of at most 0.00019.
Values sent between devices are 32-bit elements; how exact they have to be, the bound alone decides.
A program may use at most 128 MiB of HBM per device.

v0:
```python
import jax
import jax.numpy as jnp
from jax import lax
from jax.sharding import PartitionSpec as P

SWEEPS = 2


def extended(cells, sides, width):
    for axis, dim in sides:
        count = lax.axis_size(axis)
        ends = count - 1
        head = lax.slice_in_dim(cells, 0, width, axis=dim)
        tail = lax.slice_in_dim(cells, cells.shape[dim] - width, cells.shape[dim], axis=dim)
        cells = jnp.concatenate(
            [
                lax.ppermute(tail, axis, [(i, (i + 1) % count) for i in range(ends)]),
                cells,
                lax.ppermute(head, axis, [((i + 1) % count, i) for i in range(ends)]),
            ],
            axis=dim,
        )
    return cells


def stencil_sum(padded):
    padded = jnp.pad(padded, ((0, 0), (0, 0), (1, 1)))
    total = padded[2:, 1:-1, 1:-1] + padded[:-2, 1:-1, 1:-1]
    total = total + padded[1:-1, 2:, 1:-1] + padded[1:-1, :-2, 1:-1]
    total = total + padded[1:-1, 1:-1, 2:] + padded[1:-1, 1:-1, :-2]
    return total


def sweep_once(field, divergence, diagonal):
    padded = extended(field, (("gx", 0), ("gy", 1)), 1)
    return (divergence + stencil_sum(padded)) / (6.0 + diagonal)


def shards(
    pressure, divergence, diagonal, normals, traction, slot_of, counts, previous, secant_v, secant_w
):
    columns = secant_v.shape[0]
    capacity = previous.shape[1]
    slot_index = jnp.arange(capacity, dtype=jnp.int32)
    occupied = (slot_index < counts[0]).astype(jnp.float32)
    masked_v = (secant_v * occupied[None, None, :]).reshape(columns, 3 * capacity)
    gram_local = jnp.dot(masked_v, masked_v.T, precision=lax.Precision.HIGHEST)
    field = pressure
    for sweep_index in range(SWEEPS):
        field = sweep_once(field, divergence, diagonal)
    surface = field[:, :, -1].reshape(-1)
    forces = normals * surface[None, :] + traction
    own_index = lax.axis_index("gy")
    all_slots = slot_of[0]
    gathered = lax.all_gather(forces, "gy", axis=1, tiled=True)
    placed = jnp.where(all_slots // capacity == own_index, all_slots % capacity, capacity)
    owned = jnp.zeros((3, capacity), jnp.float32).at[:, placed].set(gathered, mode="drop")
    residual = occupied[None, :] * (owned - previous)
    projection_local = jnp.dot(
        masked_v, residual.reshape(3 * capacity), precision=lax.Precision.HIGHEST
    )
    gram, projection = lax.psum((gram_local, projection_local), ("gx", "gy"))
    factor = jnp.linalg.cholesky(gram)
    coefficient = -jax.scipy.linalg.cho_solve((factor, True), projection)
    update = jnp.dot(
        coefficient, secant_w.reshape(columns, 3 * capacity), precision=lax.Precision.HIGHEST
    ).reshape(3, capacity)
    coupled = occupied[None, :] * (owned + update)
    return (field, coupled)


def solution(mesh):
    placed = (
        P("gx", "gy", None),
        P("gx", "gy", None),
        P("gx", "gy", None),
        P(None, ("gx", "gy")),
        P(None, ("gx", "gy")),
        P("gx", None),
        P(("gx", "gy")),
        P(None, ("gx", "gy")),
        P(None, None, ("gx", "gy")),
        P(None, None, ("gx", "gy")),
    )
    return jax.shard_map(
        shards,
        mesh=mesh,
        in_specs=placed,
        out_specs=(P("gx", "gy", None), P(None, ("gx", "gy"))),
        check_vma=False,
    )
```

profile of v0, /device:TPU:1, one launch (start us, length us, event | category | flops | bytes accessed | tf_op | source)
XLA Modules:
  0.0 306.0 jit_solution(7569810159518206231)
XLA Ops:
  0.6 0.9 fusion.35
  1.6 5.1 %collective-permute-start = (f32[1,16,512]{2,0,1:T(1,128)S(1)}, f32[1,16,512]{2,0,1:T(1,128)S(1)}, u32[]{:S(2)}, u32[]{:S(2)}) collective-permute-start(f32[1,16,512]{2,0,1:T(1,128)S(1)} %copy.23), channel_id=1, source_target_pairs={{32,0},{64,32},{96,64},{128,96},{160,128},{192,160},{224,192},{33,... | collective-permute-start | bytes 98312 | tf_op jit(solution)/shard_map/ppermute | solution.py:19
  6.7 1.9 collective-permute-start.1
  8.6 2.8 copy.24
  11.6 1.4 collective-permute-start.2
  13.0 4.0 %collective-permute-start.3 = (f32[66,1,512]{2,0,1:T(8,128)S(1)}, f32[66,1,512]{2,0,1:T(8,128)S(1)}, u32[]{:S(2)}, u32[]{:S(2)}) collective-permute-start(f32[66,1,512]{2,0,1:T(8,128)S(1)} %get-tuple-element.12), channel_id=1, source_target_pairs={{0,1},{1,2},{2,3},{3,4},{4,5},{5,6},{6,7},{7,8},{8,9},{9,10},{10,1... | collective-permute-start | bytes 405512 | tf_op jit(solution)/shard_map/ppermute | solution.py:17
  17.0 1.8 compare_select_fusion
  19.5 2.8 select_maximum_fusion.4
  22.4 6.9 %fusion.7 = f32[64,16,512]{2,0,1:T(8,128)S(1)} fusion(f32[66,18,514]{2,0,1:T(8,128)S(1)} %select_maximum_fusion.4, f32[66,1,512]{2,0,1:T(8,128)S(1)} %collective-permute-done.3, f32[1,16,512]{2,0,1:T(1,128)S(1)} %collective-permute-done, f32[64,16,512]{2,0,1:T(8,128)} %copy-done.1, f32[1,16,512]{2,0,1:T(1,128)S(1)} %collective-permute-done.1, ...), kind=kLoop, calls=%fused_computation.29 | loop fusion | flops 8388608 | bytes 12918784 | tf_op jit(solution)/shard_map/div | solution.py:36
  29.3 3.4 %collective-permute-start.4 = (f32[1,16,512]{2,0,1:T(1,128)S(1)}, f32[1,16,512]{2,0,1:T(1,128)S(1)}, u32[]{:S(2)}, u32[]{:S(2)}) collective-permute-start(f32[1,16,512]{2,0,1:T(1,128)S(1)} %get-tuple-element.15), channel_id=1, source_target_pairs={{32,0},{64,32},{96,64},{128,96},{160,128},{192,160},{224,192},{33,... | collective-permute-start | bytes 98312 | tf_op jit(solution)/shard_map/ppermute | solution.py:19
  32.8 2.6 collective-permute-start.5
  35.4 1.7 copy.35
  37.1 1.4 collective-permute-start.6
  38.5 4.9 %collective-permute-start.7 = (f32[66,1,512]{2,0,1:T(8,128)S(1)}, f32[66,1,512]{2,0,1:T(8,128)S(1)}, u32[]{:S(2)}, u32[]{:S(2)}) collective-permute-start(f32[66,1,512]{2,0,1:T(8,128)S(1)} %get-tuple-element.10), channel_id=1, source_target_pairs={{0,1},{1,2},{2,3},{3,4},{4,5},{5,6},{6,7},{7,8},{8,9},{9,10},{10,1... | collective-permute-start | bytes 405512 | tf_op jit(solution)/shard_map/ppermute | solution.py:17
  43.5 1.1 convolution_bitcast_fusion
  44.6 1.1 collective-permute-done.6
  45.7 0.9 collective-permute-done.7
  46.6 2.8 select_maximum_fusion
  49.5 6.7 %fusion.2 = f32[64,16,512]{2,0,1:T(8,128)S(1)} fusion(f32[66,18,514]{2,0,1:T(8,128)S(1)} %select_maximum_fusion, f32[66,1,512]{2,0,1:T(8,128)S(1)} %collective-permute-done.7, f32[1,16,512]{2,0,1:T(1,128)S(1)} %collective-permute-done.4, f32[64,16,512]{2,0,1:T(8,128)S(1)} %fusion.7, f32[1,16,512]{2,0,1:T(1,128)S(1)} %collective-permute-done.5, ...), kind=kLoop, calls=%fused_computation.14 | loop fusion | flops 8388608 | bytes 12918784 | tf_op jit(solution)/shard_map/div | solution.py:36
  56.4 2.5 copy.37
  59.6 48.0 %all_gather.3 = f32[3,32768]{1,0:T(4,128)S(1)} all-gather(f32[3,1024]{1,0:T(4,128)S(1)} %multiply_add_fusion), channel_id=1, replica_groups=mesh['gx'=8,'gy'=32] {'gy'}, dimensions={1}, use_global_device_ids=true | all-gather | bytes 405504 | tf_op jit(solution)/shard_map/all_gather | solution.py:55
  107.6 8.5 %copy.32 = f32[32768,3]{1,0:T(8,128)} copy(f32[32768,3]{0,1:T(4,128)S(1)} %bitcast.77) | data formatting | bytes 786432 | tf_op jit(solution)/shard_map/all_gather | solution.py:55
  116.1 80.8 %scatter_custom_fusion = f32[3,3072]{0,1:T(8,128)S(1)} fusion(s32[32768]{0:T(1024)} %bitcast.78, f32[32768,3]{1,0:T(8,128)} %copy.32, f32[]{:T(128)} %constant.70.clone.1), kind=kCustom, calls=%fused_computation.58 | custom fusion | bytes 37376 | tf_op jit(solution)/shard_map/scatter | solution.py:57
  196.9 3.0 multiply_bitcast_fusion
  200.0 1.9 copy.40
  201.8 2.3 fusion.20
  204.1 86.8 %all-reduce.2 = (f32[32,32]{0,1:T(8,128)S(1)}, f32[32]{0:T(128)S(1)}) all-reduce(f32[32,32]{0,1:T(8,128)S(1)} %convolution_bitcast_fusion, f32[32]{0:T(128)S(1)} %fusion.20), channel_id=1, replica_groups=mesh['gx'=8,'gy'=32] {'gx','gy'}, use_global_device_ids=true, to_apply=%region_1.2 | all-reduce | flops 1056 | bytes 8448 | tf_op jit(solution)/shard_map/psum | solution.py:62
  291.1 2.9 cholesky.16
  295.3 2.4 custom-call.10
  298.7 1.7 copy.42
  300.4 3.0 fusion.11
  303.5 2.5 copy.38
  (46 shorter events, 3.4 us)
Async XLA Ops:
  0.6 297.4 %copy-start = (f32[32,3,3072]{2,0,1:T(8,128)S(1)}, f32[32,3,3072]{2,0,1:T(8,128)}, u32[]{:S(2)}) copy-start(f32[32,3,3072]{2,0,1:T(8,128)} %param.19) | copy-start | bytes 3538948
  1.6 9.9 %collective-permute-start = (f32[1,16,512]{2,0,1:T(1,128)S(1)}, f32[1,16,512]{2,0,1:T(1,128)S(1)}, u32[]{:S(2)}, u32[]{:S(2)}) collective-permute-start(f32[1,16,512]{2,0,1:T(1,128)S(1)} %copy.23), channel_id=1, source_target_pairs={{32,0},{64,32},{96,64},{128,96},{160,128},{192,160},{224,192},{33,... | collective-permute-start | bytes 98312 | tf_op jit(solution)/shard_map/ppermute | solution.py:19
  6.7 4.8 %collective-permute-start.1 = (f32[1,16,512]{2,0,1:T(1,128)S(1)}, f32[1,16,512]{2,0,1:T(1,128)S(1)}, u32[]{:S(2)}, u32[]{:S(2)}) collective-permute-start(f32[1,16,512]{2,0,1:T(1,128)S(1)} %copy.25), channel_id=1, source_target_pairs={{0,32},{32,64},{64,96},{96,128},{128,160},{160,192},{192,224},{1,3... | collective-permute-start | bytes 98312 | tf_op jit(solution)/shard_map/ppermute | solution.py:17
  11.5 8.0 %copy-start.1 = (f32[64,16,512]{2,0,1:T(8,128)}, f32[64,16,512]{2,0,1:T(8,128)S(1)}, u32[]{:S(2)}) copy-start(f32[64,16,512]{2,0,1:T(8,128)S(1)} %copy.24) | copy-start | bytes 6291460
  11.5 5.5 %copy-start.7 = (s32[1,32768]{1,0:T(1,128)S(1)}, s32[1,32768]{1,0:T(1,128)}, u32[]{:S(2)}) copy-start(s32[1,32768]{1,0:T(1,128)} %param.15) | copy-start | bytes 393220
  11.6 7.9 %collective-permute-start.2 = (f32[66,1,512]{2,0,1:T(8,128)S(1)}, f32[66,1,512]{2,0,1:T(8,128)S(1)}, u32[]{:S(2)}, u32[]{:S(2)}) collective-permute-start(f32[66,1,512]{2,0,1:T(8,128)S(1)} %get-tuple-element.13), channel_id=1, source_target_pairs={{1,0},{2,1},{3,2},{4,3},{5,4},{6,5},{7,6},{8,7},{9,8},{10,9},{11,1... | collective-permute-start | bytes 405512 | tf_op jit(solution)/shard_map/ppermute | solution.py:19
  13.0 6.5 %collective-permute-start.3 = (f32[66,1,512]{2,0,1:T(8,128)S(1)}, f32[66,1,512]{2,0,1:T(8,128)S(1)}, u32[]{:S(2)}, u32[]{:S(2)}) collective-permute-start(f32[66,1,512]{2,0,1:T(8,128)S(1)} %get-tuple-element.12), channel_id=1, source_target_pairs={{0,1},{1,2},{2,3},{3,4},{4,5},{5,6},{6,7},{7,8},{8,9},{9,10},{10,1... | collective-permute-start | bytes 405512 | tf_op jit(solution)/shard_map/ppermute | solution.py:17
  19.4 2.9 copy-start.2
  19.5 2.9 copy-start.4
  22.4 13.0 %copy-start.8 = (f32[3,3072]{1,0:T(4,128)S(1)}, f32[3,3072]{1,0:T(4,128)}, u32[]{:S(2)}) copy-start(f32[3,3072]{1,0:T(4,128)} %param.17) | copy-start | bytes 110596
  29.3 7.7 %collective-permute-start.4 = (f32[1,16,512]{2,0,1:T(1,128)S(1)}, f32[1,16,512]{2,0,1:T(1,128)S(1)}, u32[]{:S(2)}, u32[]{:S(2)}) collective-permute-start(f32[1,16,512]{2,0,1:T(1,128)S(1)} %get-tuple-element.15), channel_id=1, source_target_pairs={{32,0},{64,32},{96,64},{128,96},{160,128},{192,160},{224,192},{33,... | collective-permute-start | bytes 98312 | tf_op jit(solution)/shard_map/ppermute | solution.py:19
  32.8 4.3 %collective-permute-start.5 = (f32[1,16,512]{2,0,1:T(1,128)S(1)}, f32[1,16,512]{2,0,1:T(1,128)S(1)}, u32[]{:S(2)}, u32[]{:S(2)}) collective-permute-start(f32[1,16,512]{2,0,1:T(1,128)S(1)} %get-tuple-element.14), channel_id=1, source_target_pairs={{0,32},{32,64},{64,96},{96,128},{128,160},{160,192},{192,224},{1,3... | collective-permute-start | bytes 98312 | tf_op jit(solution)/shard_map/ppermute | solution.py:17
  37.0 6.4 %copy-start.6 = (f32[32,3,3072]{2,0,1:T(8,128)S(1)}, f32[32,3,3072]{2,0,1:T(8,128)}, u32[]{:S(2)}) copy-start(f32[32,3,3072]{2,0,1:T(8,128)} %param.18) | copy-start | bytes 3538948
  37.1 8.6 %collective-permute-start.6 = (f32[66,1,512]{2,0,1:T(8,128)S(1)}, f32[66,1,512]{2,0,1:T(8,128)S(1)}, u32[]{:S(2)}, u32[]{:S(2)}) collective-permute-start(f32[66,1,512]{2,0,1:T(8,128)S(1)} %get-tuple-element.11), channel_id=1, source_target_pairs={{1,0},{2,1},{3,2},{4,3},{5,4},{6,5},{7,6},{8,7},{9,8},{10,9},{11,1... | collective-permute-start | bytes 405512 | tf_op jit(solution)/shard_map/ppermute | solution.py:19
  38.5 8.1 %collective-permute-start.7 = (f32[66,1,512]{2,0,1:T(8,128)S(1)}, f32[66,1,512]{2,0,1:T(8,128)S(1)}, u32[]{:S(2)}, u32[]{:S(2)}) collective-permute-start(f32[66,1,512]{2,0,1:T(8,128)S(1)} %get-tuple-element.10), channel_id=1, source_target_pairs={{0,1},{1,2},{2,3},{3,4},{4,5},{5,6},{6,7},{7,8},{8,9},{9,10},{10,1... | collective-permute-start | bytes 405512 | tf_op jit(solution)/shard_map/ppermute | solution.py:17
  44.5 4.9 %copy-start.3 = (f32[64,16,512]{2,1,0:T(8,128)S(1)}, f32[64,16,512]{2,1,0:T(8,128)}, u32[]{:S(2)}) copy-start(f32[64,16,512]{2,1,0:T(8,128)} %param.11) | copy-start | bytes 6291460
  44.6 4.9 %copy-start.5 = (f32[64,16,512]{2,1,0:T(8,128)S(1)}, f32[64,16,512]{2,1,0:T(8,128)}, u32[]{:S(2)}) copy-start(f32[64,16,512]{2,1,0:T(8,128)} %param.12) | copy-start | bytes 6291460
  56.4 3.1 %copy-start.9 = (f32[3,1024]{1,0:T(4,128)S(1)}, f32[3,1024]{1,0:T(4,128)}, u32[]{:S(2)}) copy-start(f32[3,1024]{1,0:T(4,128)} %param.14) | copy-start | bytes 36868
  56.4 3.1 %copy-start.10 = (f32[3,1024]{1,0:T(4,128)S(1)}, f32[3,1024]{1,0:T(4,128)}, u32[]{:S(2)}) copy-start(f32[3,1024]{1,0:T(4,128)} %param.13) | copy-start | bytes 36868
where the time goes:
time: 307 us; the launch traced here: 306 us
  blocking collectives  135 us (44%)
  local copies, waits for them, and re-layouts  104 us (34%)
  other arithmetic  33.9 us (11%)
  starting transfers between devices  24.8 us (8%)
  matrix products  4.35 us (1%)
    psum x1, blocking collectives, shards(): gram, projection = lax.psum((gram_local, projection_local), ('gx', 'gy'))  86.8 us
    scatter x1, local copies, waits for them, and re-layouts, shards(): jnp.zeros((3, capacity), jnp.float32).at[:, placed]  80.8 us
    all_gather x1, blocking collectives, shards(): gathered = lax.all_gather(forces, 'gy', axis=1, tiled=True)  48 us
    div x2, other arithmetic, sweep_once(): return (divergence + stencil_sum(padded)) / (6.0 + diagonal)  13.6 us
    ppermute x4, starting transfers between devices, extended(): lax.ppermute(tail, axis, [(i, (i + 1) % count) for i in range(ends)])  13.4 us
    ppermute x4, starting transfers between devices, extended(): lax.ppermute(head, axis, [((i + 1) % count, i) for i in range(ends)])  11.4 us
    unnamed x26, local copies, waits for them, and re-layouts  9.59 us
    all_gather x1, local copies, waits for them, and re-layouts, shards(): gathered = lax.all_gather(forces, 'gy', axis=1, tiled=True)  8.53 us
  transfers between devices with their start and end apart: 8, of which 2 were waited for; matrix products, arithmetic and copies ran while one was open for 2% of the time, Pallas kernels for 0%

commit v1 on v0

--- a/solution.py
+++ b/solution.py
@@ -52,7 +52,11 @@
     forces = normals * surface[None, :] + traction
     own_index = lax.axis_index("gy")
     all_slots = slot_of[0]
-    gathered = lax.all_gather(forces, "gy", axis=1, tiled=True)
+    windows = []
+    for _ in range(lax.axis_size("gy")):
+        windows.append(forces)
+    local_part = jnp.concatenate(windows, axis=1)
+    gathered = lax.all_to_all(local_part, axis_name="gy", split_axis=1, concat_axis=1, tiled=True)
     placed = jnp.where(all_slots // capacity == own_index, all_slots % capacity, capacity)
     owned = jnp.zeros((3, capacity), jnp.float32).at[:, placed].set(gathered, mode="drop")
     residual = occupied[None, :] * (owned - previous)

time: 307 us -> 281 us (0.915)
  blocking collectives: 135 us -> 74.8 us
  starting transfers between devices: 24.8 us -> 42.9 us
  waiting for transfers between devices: 2.07 us -> 13.4 us
  local copies, waits for them, and re-layouts: 104 us -> 108 us
    all_gather x1 -> x0, blocking collectives: 48 us -> none  [shards(): gathered = lax.all_gather(forces, 'gy', axis=1, tiled=True)]
    all_to_all x0 -> x1, starting transfers between devices: none -> 17.6 us  [shards(): lax.all_to_all(local_part, axis_name='gy', split_axis=1, concat_axis=1, t...]
    psum x1, blocking collectives: 86.8 us -> 74.8 us  [shards(): gram, projection = lax.psum((gram_local, projection_local), ('gx', 'gy'))]
    all_to_all x0 -> x1, local copies, waits for them, and re-layouts: none -> 9.07 us  [shards(): lax.all_to_all(local_part, axis_name='gy', split_axis=1, concat_axis=1, t...]
    all_gather x1 -> x0, local copies, waits for them, and re-layouts: 8.53 us -> none  [shards(): gathered = lax.all_gather(forces, 'gy', axis=1, tiled=True)]
    all_to_all x0 -> x1, waiting for transfers between devices: none -> 6.87 us  [shards(): lax.all_to_all(local_part, axis_name='gy', split_axis=1, concat_axis=1, t...]
    unnamed x26 -> x56, local copies, waits for them, and re-layouts: 9.59 us -> 12.8 us
  transfers between devices with their start and end apart: 8 -> 9, of which waited for: 2 -> 6; matrix products, arithmetic and copies ran while one was open for 2% -> 4% of each run, Pallas kernels for 0% -> 0%
where the time goes in v1:
time: 281 us
  local copies, waits for them, and re-layouts  108 us (38%)
  blocking collectives  74.8 us (27%)
  starting transfers between devices  42.9 us (15%)
  other arithmetic  33.4 us (12%)
  waiting for transfers between devices  13.4 us (5%)
  matrix products  6.17 us (2%)
    scatter x1, local copies, waits for them, and re-layouts, shards(): jnp.zeros((3, capacity), jnp.float32).at[:, placed]  80.8 us
    psum x1, blocking collectives, shards(): gram, projection = lax.psum((gram_local, projection_local), ('gx', 'gy'))  74.8 us
    all_to_all x1, starting transfers between devices, shards(): lax.all_to_all(local_part, axis_name='gy', split_axis=1, concat_axis=1, t...  17.6 us
    ppermute x4, starting transfers between devices, extended(): lax.ppermute(tail, axis, [(i, (i + 1) % count) for i in range(ends)])  14.2 us
    unnamed x56, local copies, waits for them, and re-layouts  12.8 us
    div x2, other arithmetic, sweep_once(): return (divergence + stencil_sum(padded)) / (6.0 + diagonal)  12.2 us
    ppermute x4, starting transfers between devices, extended(): lax.ppermute(head, axis, [((i + 1) % count, i) for i in range(ends)])  11.2 us
    all_to_all x1, local copies, waits for them, and re-layouts, shards(): lax.all_to_all(local_part, axis_name='gy', split_axis=1, concat_axis=1, t...  9.07 us
  transfers between devices with their start and end apart: 9, of which 6 were waited for; matrix products, arithmetic and copies ran while one was open for 4% of the time, Pallas kernels for 0%

profile of v1, /device:TPU:1, one launch (start us, length us, event | category | flops | bytes accessed | tf_op | source)
XLA Modules:
  0.0 280.6 jit_solution(15479778463238182518)
XLA Ops:
  1.6 5.1 %collective-permute-start = (f32[1,16,512]{2,0,1:T(1,128)S(1)}, f32[1,16,512]{2,0,1:T(1,128)S(1)}, u32[]{:S(2)}, u32[]{:S(2)}) collective-permute-start(f32[1,16,512]{2,0,1:T(1,128)S(1)} %copy.38), channel_id=1, source_target_pairs={{32,0},{64,32},{96,64},{128,96},{160,128},{192,160},{224,192},{33,... | collective-permute-start | bytes 98312 | tf_op jit(solution)/shard_map/ppermute | solution.py:19
  6.7 1.9 collective-permute-start.1
  8.6 2.8 %copy.39 = f32[64,16,512]{2,0,1:T(8,128)S(1)} copy(f32[64,16,512]{2,1,0:T(8,128)} %param.10) | data formatting | bytes 4194304 | tf_op args[0]
  11.5 1.3 collective-permute-start.2
  12.8 4.3 %collective-permute-start.3 = (f32[66,1,512]{2,0,1:T(8,128)S(1)}, f32[66,1,512]{2,0,1:T(8,128)S(1)}, u32[]{:S(2)}, u32[]{:S(2)}) collective-permute-start(f32[66,1,512]{2,0,1:T(8,128)S(1)} %get-tuple-element.16), channel_id=1, source_target_pairs={{0,1},{1,2},{2,3},{3,4},{4,5},{5,6},{6,7},{7,8},{8,9},{9,10},{10,1... | collective-permute-start | bytes 405512 | tf_op jit(solution)/shard_map/ppermute | solution.py:17
  19.5 2.8 %select_maximum_fusion.4 = f32[66,18,514]{2,0,1:T(8,128)S(1)} fusion(f32[66,1,512]{2,0,1:T(8,128)S(1)} %collective-permute-done.2, f32[66,1,512]{2,0,1:T(8,128)S(1)} %collective-permute-done.3, f32[1,16,512]{2,0,1:T(1,128)S(1)} %collective-permute-done, f32[64,16,512]{2,0,1:T(8,128)S(1)} %copy.39, f32[1,16,512]{2,0,1:T(1,128)S(1)} %collective-permute-done.1), kind=kLoop, calls=%fused_computation.7 | loop fusion | flops 7327584 | bytes 4875552 | tf_op jit(solution)/shard_map/concatenate | solution.py:15
  22.4 6.8 %fusion.7 = f32[64,16,512]{2,0,1:T(8,128)S(1)} fusion(f32[66,18,514]{2,0,1:T(8,128)S(1)} %select_maximum_fusion.4, f32[66,1,512]{2,0,1:T(8,128)S(1)} %collective-permute-done.3, f32[1,16,512]{2,0,1:T(1,128)S(1)} %collective-permute-done, f32[64,16,512]{2,0,1:T(8,128)S(1)} %copy.39, f32[1,16,512]{2,0,1:T(1,128)S(1)} %collective-permute-done.1, ...), kind=kLoop, calls=%fused_computation.29 | loop fusion | flops 8388608 | bytes 12918784 | tf_op jit(solution)/shard_map/div | solution.py:36
  29.3 3.5 %collective-permute-start.4 = (f32[1,16,512]{2,0,1:T(1,128)S(1)}, f32[1,16,512]{2,0,1:T(1,128)S(1)}, u32[]{:S(2)}, u32[]{:S(2)}) collective-permute-start(f32[1,16,512]{2,0,1:T(1,128)S(1)} %get-tuple-element.19), channel_id=1, source_target_pairs={{32,0},{64,32},{96,64},{128,96},{160,128},{192,160},{224,192},{33,... | collective-permute-start | bytes 98312 | tf_op jit(solution)/shard_map/ppermute | solution.py:19
  32.8 2.6 collective-permute-start.5
  37.1 1.3 collective-permute-start.6
  38.4 5.4 %collective-permute-start.7 = (f32[66,1,512]{2,0,1:T(8,128)}, f32[66,1,512]{2,0,1:T(8,128)}, u32[]{:S(2)}, u32[]{:S(2)}) collective-permute-start(f32[66,1,512]{2,0,1:T(8,128)} %get-tuple-element.14), channel_id=1, source_target_pairs={{0,1},{1,2},{2,3},{3,4},{4,5},{5,6},{6,7},{7,8},{8,9},{9,10},{10,1... | collective-permute-start | bytes 405512 | tf_op jit(solution)/shard_map/ppermute | solution.py:17
  43.8 1.7 collective-permute-done.6
  45.6 1.4 collective-permute-done.7
  47.0 3.6 %select_maximum_fusion = f32[66,18,514]{2,0,1:T(8,128)S(1)} fusion(f32[66,1,512]{2,0,1:T(8,128)S(1)} %collective-permute-done.6, f32[66,1,512]{2,0,1:T(8,128)} %collective-permute-done.7, f32[1,16,512]{2,0,1:T(1,128)S(1)} %collective-permute-done.4, f32[64,16,512]{2,0,1:T(8,128)S(1)} %fusion.7, f32[1,16,512]{2,0,1:T(1,128)S(1)} %collective-permute-done.5), kind=kLoop, calls=%fused_computation.3 | loop fusion | flops 7327584 | bytes 4875552 | tf_op jit(solution)/shard_map/concatenate | solution.py:15
  50.7 5.4 %fusion.2 = f32[64,16,512]{2,0,1:T(8,128)S(1)} fusion(f32[66,18,514]{2,0,1:T(8,128)S(1)} %select_maximum_fusion, f32[66,1,512]{2,0,1:T(8,128)} %collective-permute-done.7, f32[1,16,512]{2,0,1:T(1,128)S(1)} %collective-permute-done.4, f32[64,16,512]{2,0,1:T(8,128)S(1)} %fusion.7, f32[1,16,512]{2,0,1:T(1,128)S(1)} %collective-permute-done.5, ...), kind=kLoop, calls=%fused_computation.14 | loop fusion | flops 8388608 | bytes 12918784 | tf_op jit(solution)/shard_map/div | solution.py:36
  56.0 1.3 copy-done.1
  59.5 17.6 %all-to-all-start = ((f32[3,32,1024]{2,0,1:T(4,128)}), f32[3,32,1024]{2,0,1:T(4,128)}, u32[]{:S(2)}, u32[]{:S(2)}) async-start(f32[3,32,1024]{2,0,1:T(4,128)} %bitcast.80), calls=%async_computation | async-start | bytes 1048576 | tf_op jit(solution)/shard_map/all_to_all | solution.py:59
  78.9 2.5 copy.50
  81.3 2.9 %convolution_bitcast_fusion = f32[32,32]{0,1:T(8,128)S(1)} fusion(f32[32,3,3072]{2,0,1:T(8,128)} %param.18, f32[3072]{0:T(1024)S(1)} %fusion.32), kind=kOutput, calls=%fused_computation.49 | convolution fusion | flops 113541120 | bytes 1196032 | tf_op jit(solution)/shard_map/dot_general | solution.py:47
  84.3 2.5 copy.52
  86.8 6.9 %all-to-all-done = f32[3,32,1024]{2,0,1:T(4,128)} async-done(((f32[3,32,1024]{2,0,1:T(4,128)}), f32[3,32,1024]{2,0,1:T(4,128)}, u32[]{:S(2)}, u32[]{:S(2)}) %all-to-all-start) | async-done | bytes 393248 | tf_op jit(solution)/shard_map/all_to_all | solution.py:59
  93.7 9.1 %copy.47 = f32[32768,3]{1,0:T(8,128)} copy(f32[32768,3]{0,1:T(4,128)} %bitcast.7) | data formatting | bytes 786432 | tf_op jit(solution)/shard_map/all_to_all | solution.py:59
  102.7 80.8 %scatter_custom_fusion = f32[3,3072]{0,1:T(8,128)S(1)} fusion(s32[32768]{0:T(1024)S(1)} %bitcast.81, f32[32768,3]{1,0:T(8,128)} %copy.47, f32[]{:T(128)} %constant.70.clone.1), kind=kCustom, calls=%fused_computation.58 | custom fusion | bytes 37376 | tf_op jit(solution)/shard_map/scatter | solution.py:61
  183.6 3.1 %multiply_bitcast_fusion = f32[3,3072,1]{0,1,2:T(8,128)} fusion(f32[3,3072]{0,1:T(8,128)S(1)} %scatter_custom_fusion, f32[3,3072]{0,1:T(8,128)} %copy.50, f32[3072]{0:T(1024)S(1)} %fusion.32), kind=kLoop, calls=%fused_computation.45 | loop fusion | flops 18432 | bytes 122880 | tf_op jit(solution)/shard_map/mul | solution.py:62
  186.6 1.9 copy.55
  188.5 2.3 fusion.20
  190.8 74.8 %all-reduce.2 = (f32[32,32]{0,1:T(8,128)S(1)}, f32[32]{0:T(128)S(1)}) all-reduce(f32[32,32]{0,1:T(8,128)S(1)} %convolution_bitcast_fusion, f32[32]{0:T(128)S(1)} %fusion.20), channel_id=1, replica_groups=mesh['gx'=8,'gy'=32] {'gx','gy'}, use_global_device_ids=true, to_apply=%region_1.2 | all-reduce | flops 1056 | bytes 8448 | tf_op jit(solution)/shard_map/psum | solution.py:66
  265.7 2.9 %cholesky.16 = f32[32,32]{1,0:T(8,128)S(1)} custom-call(f32[32,32]{1,0:T(8,128)S(1)} %fusion.31), custom_call_target="Cholesky" | custom-call | tf_op jit(solution)/shard_map/jit(cholesky)/cholesky | solution.py:67
  269.9 2.4 custom-call.10
  273.3 1.7 copy.57
  275.0 3.1 %fusion.11 = f32[3,3072]{0,1:T(8,128)} fusion(f32[3,3072]{0,1:T(8,128)S(1)} %scatter_custom_fusion, f32[1,3,3072]{1,2,0:T(8,128)} %copy.57, f32[3072]{0:T(1024)S(1)} %fusion.32), kind=kLoop, calls=%fused_computation.44 | loop fusion | flops 18432 | bytes 122880 | tf_op jit(solution)/shard_map/mul | solution.py:72
  278.1 2.5 copy.53
  (78 shorter events, 10.7 us)
Async XLA Ops:
  0.6 272.0 %copy-start = (f32[32,3,3072]{2,0,1:T(8,128)S(1)}, f32[32,3,3072]{2,0,1:T(8,128)}, u32[]{:S(2)}) copy-start(f32[32,3,3072]{2,0,1:T(8,128)} %param.19) | copy-start | bytes 3538948
  1.6 9.9 %collective-permute-start = (f32[1,16,512]{2,0,1:T(1,128)S(1)}, f32[1,16,512]{2,0,1:T(1,128)S(1)}, u32[]{:S(2)}, u32[]{:S(2)}) collective-permute-start(f32[1,16,512]{2,0,1:T(1,128)S(1)} %copy.38), channel_id=1, source_target_pairs={{32,0},{64,32},{96,64},{128,96},{160,128},{192,160},{224,192},{33,... | collective-permute-start | bytes 98312 | tf_op jit(solution)/shard_map/ppermute | solution.py:19
  6.7 4.8 %collective-permute-start.1 = (f32[1,16,512]{2,0,1:T(1,128)S(1)}, f32[1,16,512]{2,0,1:T(1,128)S(1)}, u32[]{:S(2)}, u32[]{:S(2)}) collective-permute-start(f32[1,16,512]{2,0,1:T(1,128)S(1)} %copy.40), channel_id=1, source_target_pairs={{0,32},{32,64},{64,96},{96,128},{128,160},{160,192},{192,224},{1,3... | collective-permute-start | bytes 98312 | tf_op jit(solution)/shard_map/ppermute | solution.py:17
  11.5 6.8 %collective-permute-start.2 = (f32[66,1,512]{2,0,1:T(8,128)S(1)}, f32[66,1,512]{2,0,1:T(8,128)S(1)}, u32[]{:S(2)}, u32[]{:S(2)}) collective-permute-start(f32[66,1,512]{2,0,1:T(8,128)S(1)} %get-tuple-element.17), channel_id=1, source_target_pairs={{1,0},{2,1},{3,2},{4,3},{5,4},{6,5},{7,6},{8,7},{9,8},{10,9},{11,1... | collective-permute-start | bytes 405512 | tf_op jit(solution)/shard_map/ppermute | solution.py:19
  12.8 9.5 %copy-start.3 = (f32[64,16,512]{2,1,0:T(8,128)S(1)}, f32[64,16,512]{2,1,0:T(8,128)}, u32[]{:S(2)}) copy-start(f32[64,16,512]{2,1,0:T(8,128)} %param.11) | copy-start | bytes 6291460
  12.8 9.5 %copy-start.5 = (f32[64,16,512]{2,1,0:T(8,128)S(1)}, f32[64,16,512]{2,1,0:T(8,128)}, u32[]{:S(2)}) copy-start(f32[64,16,512]{2,1,0:T(8,128)} %param.12) | copy-start | bytes 6291460
  12.8 6.7 %collective-permute-start.3 = (f32[66,1,512]{2,0,1:T(8,128)S(1)}, f32[66,1,512]{2,0,1:T(8,128)S(1)}, u32[]{:S(2)}, u32[]{:S(2)}) collective-permute-start(f32[66,1,512]{2,0,1:T(8,128)S(1)} %get-tuple-element.16), channel_id=1, source_target_pairs={{0,1},{1,2},{2,3},{3,4},{4,5},{5,6},{6,7},{7,8},{8,9},{9,10},{10,1... | collective-permute-start | bytes 405512 | tf_op jit(solution)/shard_map/ppermute | solution.py:17
  29.3 6.1 %collective-permute-start.4 = (f32[1,16,512]{2,0,1:T(1,128)S(1)}, f32[1,16,512]{2,0,1:T(1,128)S(1)}, u32[]{:S(2)}, u32[]{:S(2)}) collective-permute-start(f32[1,16,512]{2,0,1:T(1,128)S(1)} %get-tuple-element.19), channel_id=1, source_target_pairs={{32,0},{64,32},{96,64},{128,96},{160,128},{192,160},{224,192},{33,... | collective-permute-start | bytes 98312 | tf_op jit(solution)/shard_map/ppermute | solution.py:19
  32.8 3.6 %collective-permute-start.5 = (f32[1,16,512]{2,0,1:T(1,128)S(1)}, f32[1,16,512]{2,0,1:T(1,128)S(1)}, u32[]{:S(2)}, u32[]{:S(2)}) collective-permute-start(f32[1,16,512]{2,0,1:T(1,128)S(1)} %get-tuple-element.18), channel_id=1, source_target_pairs={{0,32},{32,64},{64,96},{96,128},{128,160},{160,192},{192,224},{1,3... | collective-permute-start | bytes 98312 | tf_op jit(solution)/shard_map/ppermute | solution.py:17
  37.1 8.4 %collective-permute-start.6 = (f32[66,1,512]{2,0,1:T(8,128)}, f32[66,1,512]{2,0,1:T(8,128)S(1)}, u32[]{:S(2)}, u32[]{:S(2)}) collective-permute-start(f32[66,1,512]{2,0,1:T(8,128)} %get-tuple-element.15), channel_id=1, source_target_pairs={{1,0},{2,1},{3,2},{4,3},{5,4},{6,5},{7,6},{8,7},{9,8},{10,9},{11,1... | collective-permute-start | bytes 405512 | tf_op jit(solution)/shard_map/ppermute | solution.py:19
  38.4 8.6 %collective-permute-start.7 = (f32[66,1,512]{2,0,1:T(8,128)}, f32[66,1,512]{2,0,1:T(8,128)}, u32[]{:S(2)}, u32[]{:S(2)}) collective-permute-start(f32[66,1,512]{2,0,1:T(8,128)} %get-tuple-element.14), channel_id=1, source_target_pairs={{0,1},{1,2},{2,3},{3,4},{4,5},{5,6},{6,7},{7,8},{8,9},{9,10},{10,1... | collective-permute-start | bytes 405512 | tf_op jit(solution)/shard_map/ppermute | solution.py:17
  43.8 6.8 %copy-start.4 = (f32[64,16,512]{2,1,0:T(8,128)S(1)}, f32[64,16,512]{2,1,0:T(8,128)}, u32[]{:S(2)}) copy-start(f32[64,16,512]{2,1,0:T(8,128)} %param.11) | copy-start | bytes 6291460
  43.8 6.8 %copy-start.6 = (f32[64,16,512]{2,1,0:T(8,128)S(1)}, f32[64,16,512]{2,1,0:T(8,128)}, u32[]{:S(2)}) copy-start(f32[64,16,512]{2,1,0:T(8,128)} %param.12) | copy-start | bytes 6291460
  50.6 7.5 %copy-start.9 = (f32[3,1024]{1,0:T(4,128)S(1)}, f32[3,1024]{1,0:T(4,128)}, u32[]{:S(2)}) copy-start(f32[3,1024]{1,0:T(4,128)} %param.14) | copy-start | bytes 36868
  50.7 7.5 %copy-start.10 = (f32[3,1024]{1,0:T(4,128)S(1)}, f32[3,1024]{1,0:T(4,128)}, u32[]{:S(2)}) copy-start(f32[3,1024]{1,0:T(4,128)} %param.13) | copy-start | bytes 36868
  56.0 1.3 copy-start.1
  57.4 19.7 %copy-start.8 = (s32[1,32768]{1,0:T(1,128)S(1)}, s32[1,32768]{1,0:T(1,128)}, u32[]{:S(2)}) copy-start(s32[1,32768]{1,0:T(1,128)} %param.15) | copy-start | bytes 393220
  58.6 25.6 %copy-start.2 = (f32[64,16,512]{2,0,1:T(8,128)S(1)}, f32[64,16,512]{2,0,1:T(8,128)}, u32[]{:S(2)}) copy-start(f32[64,16,512]{2,0,1:T(8,128)} %copy-done.1) | copy-start | bytes 6291460
  58.7 0.8 copy-start.7
  59.5 34.2 %all-to-all-start = ((f32[3,32,1024]{2,0,1:T(4,128)}), f32[3,32,1024]{2,0,1:T(4,128)}, u32[]{:S(2)}, u32[]{:S(2)}) async-start(f32[3,32,1024]{2,0,1:T(4,128)} %bitcast.80), calls=%async_computation | async-start | bytes 1048576 | tf_op jit(solution)/shard_map/all_to_all | solution.py:59
